TPU v7x, 128 devices: a whole 4x4x4 slice. The times are simulated.
128 devices in a mesh: tm: 8 (over y, x_lo), space: 16 (over z, x_hi, core).
Axes of the slice: x: 4 (x_hi: 2, x_lo: 2; x = x_hi * 2 + x_lo), y: 4, z: 4, core: 2. Of those that a mesh axis runs over, the one named last changes fastest.
Arguments:
- queries: bfloat16 [16384, 4096], P(('tm', 'space')), may hold values from -20 to 20
- key_vectors: bfloat16 [16384, 4096], P(('tm', 'space')), may hold values from -20 to 20
- value_vectors: bfloat16 [16384, 4096], P(('tm', 'space')), may hold values from -6 to 6
- out_weight: bfloat16 [4096, 6144], P(None, 'space'), may hold values from -0.375 to 0.375
- frame_mask: int32 [8, 8], replicated, may hold values 0 or 1
Outputs:
- projected: bfloat16 [16384, 6144], P('tm', 'space')
All inputs are finite; a program needn't handle non-finite values.
Results may differ from a plain program's by a relative error of at most 0.0075.
Values may be sent and summed in bfloat16 or wider, within the bound.
A program may use at most 128 MiB of HBM per device.

v0:
```python
import math

import jax
import jax.numpy as jnp
from jax import lax
from jax.sharding import PartitionSpec as P

HD = 128


def passed_along(x, axis, by):
    devices = lax.axis_size(axis)
    return lax.ppermute(x, axis, [(i, (i + by) % devices) for i in range(devices)])


def block_update(state, query_blocks, arrived, allowed, scale_factor):
    run_max, run_total, run_sum = state
    keys_here = arrived[0]
    values_here = arrived[1]

    def one_block(pieces):
        query_part, old_max, old_total, old_sum = pieces
        scores = (
            jnp.einsum("qhd,khd->qhk", query_part, keys_here, preferred_element_type=jnp.float32)
            * scale_factor
        )
        block_max = jnp.where(allowed, jnp.max(scores, axis=2), -jnp.inf)
        new_max = jnp.maximum(old_max, block_max)
        exp_terms = jnp.where(allowed, jnp.exp(scores - new_max[:, :, None]), 0.0)
        rescale = jnp.exp(old_max - new_max)
        new_total = old_total * rescale + jnp.sum(exp_terms, axis=2)
        new_sum = old_sum * rescale[:, :, None] + jnp.einsum(
            "qhk,khd->qhd",
            exp_terms.astype(jnp.bfloat16),
            values_here,
            preferred_element_type=jnp.float32,
        )
        return (new_max, new_total, new_sum)

    return lax.map(one_block, (query_blocks, run_max, run_total, run_sum))


def mask_bit(frame_mask, row_index, column_index):
    count = frame_mask.shape[0]
    grid_rows = lax.broadcasted_iota(jnp.int32, (count, count), 0)
    grid_cols = lax.broadcasted_iota(jnp.int32, (count, count), 1)
    return jnp.sum(jnp.where((grid_rows == row_index) & (grid_cols == column_index), frame_mask, 0))


def body(queries, key_vectors, value_vectors, out_weight, frame_mask):
    frames = lax.axis_size("tm")
    here = lax.axis_index("tm")
    head_queries, head_keys, head_values = (
        lax.all_to_all(queries, "space", split_axis=1, concat_axis=0, tiled=True),
        lax.all_to_all(key_vectors, "space", split_axis=1, concat_axis=0, tiled=True),
        lax.all_to_all(value_vectors, "space", split_axis=1, concat_axis=0, tiled=True),
    )
    row_count = head_queries.shape[0]
    local_heads = head_queries.shape[1] // HD
    scale_factor = 1.0 / math.sqrt(HD)
    block_rows = 512
    block_count = row_count // block_rows
    query_blocks = head_queries.reshape(block_count, block_rows, local_heads, HD)
    pair = jnp.stack([head_keys, head_values]).reshape(2, row_count, local_heads, HD)
    state = (
        jnp.full((block_count, block_rows, local_heads), -jnp.inf, jnp.float32),
        jnp.zeros((block_count, block_rows, local_heads), jnp.float32),
        jnp.zeros((block_count, block_rows, local_heads, HD), jnp.float32),
    )
    state = block_update(state, query_blocks, pair, True, scale_factor)

    def visit(current, arrived, source):
        source_block = jnp.mod(source, frames)
        granted = mask_bit(frame_mask, here, source_block) == 1
        return block_update(current, query_blocks, arrived, granted, scale_factor)

    lower = pair
    upper = pair
    lower = passed_along(lower, "tm", 1)
    upper = passed_along(upper, "tm", -1)
    state = visit(state, lower, here - 1)
    state = visit(state, upper, here + 1)
    run_max, run_total, run_sum = state
    attended = (
        (run_sum / run_total[:, :, :, None])
        .reshape(row_count, local_heads * HD)
        .astype(jnp.bfloat16)
    )
    projected = jnp.dot(
        lax.all_gather(attended, "space", axis=1, tiled=True),
        out_weight,
        preferred_element_type=jnp.float32,
    )
    return projected.astype(jnp.bfloat16)


def solution(mesh):
    in_specs = (
        P(("tm", "space"), None),
        P(("tm", "space"), None),
        P(("tm", "space"), None),
        P(None, "space"),
        P(),
    )
    out_specs = P("tm", "space")
    return jax.shard_map(body, mesh=mesh, in_specs=in_specs, out_specs=out_specs, check_vma=False)
```

profile of v0, /device:TPU:27, one launch (start us, length us, event | category | flops | bytes accessed | tf_op | source)
XLA Modules:
  0.0 363.2 jit_solution(35502770364361457)
XLA Ops:
  9.0 7.6 %all-to-all-start.1 = ((bf16[128,16,256]{0,2,1:T(8,128)(2,1)}), bf16[128,16,256]{0,2,1:T(8,128)(2,1)}, u32[]{:S(2)}, u32[]{:S(2)}) async-start(bf16[128,16,256]{0,2,1:T(8,128)(2,1)} %bitcast.265), calls=%async_computation.1 | async-start | bytes 2097152 | tf_op jit(solution)/shard_map/all_to_all | solution.py:55
  18.8 14.9 %all-to-all-done.1 = bf16[128,16,256]{0,2,1:T(8,128)(2,1)} async-done(((bf16[128,16,256]{0,2,1:T(8,128)(2,1)}), bf16[128,16,256]{0,2,1:T(8,128)(2,1)}, u32[]{:S(2)}, u32[]{:S(2)}) %all-to-all-start.1) | async-done | bytes 1048608 | tf_op jit(solution)/shard_map/all_to_all | solution.py:55
  33.7 5.1 %all-to-all-start.2 = ((bf16[128,16,256]{0,2,1:T(8,128)(2,1)}), bf16[128,16,256]{0,2,1:T(8,128)(2,1)}, u32[]{:S(2)}, u32[]{:S(2)}) async-start(bf16[128,16,256]{0,2,1:T(8,128)(2,1)} %bitcast.263), calls=%async_computation.2 | async-start | bytes 2097152 | tf_op jit(solution)/shard_map/all_to_all | solution.py:56
  41.1 15.0 %all-to-all-done.2 = bf16[128,16,256]{0,2,1:T(8,128)(2,1)} async-done(((bf16[128,16,256]{0,2,1:T(8,128)(2,1)}), bf16[128,16,256]{0,2,1:T(8,128)(2,1)}, u32[]{:S(2)}, u32[]{:S(2)}) %all-to-all-start.2) | async-done | bytes 1048608 | tf_op jit(solution)/shard_map/all_to_all | solution.py:56
  56.2 5.1 %all-to-all-start = ((bf16[128,16,256]{2,0,1:T(8,128)(2,1)}), bf16[128,16,256]{2,0,1:T(8,128)(2,1)}, u32[]{:S(2)}, u32[]{:S(2)}) async-start(bf16[128,16,256]{2,0,1:T(8,128)(2,1)} %bitcast.262), calls=%async_computation | async-start | bytes 2097152 | tf_op jit(solution)/shard_map/all_to_all | solution.py:54
  63.5 2.9 copy.21
  71.0 2.9 copy.23
  95.2 27.9 %while.40 = (s32[]{:T(128)}, f32[4,512,2]{1,2,0:T(2,128)S(1)}, f32[4,512,2]{1,2,0:T(2,128)S(1)}, f32[4,512,2,128]{3,1,2,0:T(8,128)}, bf16[4,512,2,128]{3,1,2,0:T...) while((s32[]{:T(128)}, f32[4,512,2]{1,2,0:T(2,128)S(1)}, ...), condition=%wide.region_3.4_spmd, body=%wide.region_0.3_spmd.sunk | while | flops 1090653184 | bytes 32289908 | solution.py:40
  123.1 7.3 %collective-permute-done = bf16[2,2048,2,128]{1,3,2,0:T(8,128)(2,1)} collective-permute-done((bf16[2,2048,2,128]{1,3,2,0:T(8,128)(2,1)}, bf16[2,2048,2,128]{1,3,2,0:T(8,128)(2,1)}, u32[]{:S(2)}, u32[]{:S(2)}) %collective-permute-start) | collective-permute-done | bytes 2097184 | tf_op jit(solution)/shard_map/ppermute | solution.py:13
  130.4 3.1 slice_bitcast_fusion.2
  139.5 33.0 %while.41 = (s32[]{:T(128)}, f32[4,512,2]{1,2,0:T(2,128)S(1)}, f32[4,512,2]{1,2,0:T(2,128)S(1)}, f32[4,512,2,128]{3,1,2,0:T(8,128)}, f32[4,512,2]{1,2,0:T(2,128)...) while((s32[]{:T(128)}, f32[4,512,2]{1,2,0:T(2,128)S(1)}, ...), condition=%wide.region_8.9_spmd, body=%wide.region_5.8_spmd.sunk | while | flops 1094981632 | bytes 32831132 | solution.py:40
  139.6 2.7 bitcast_reduce_fusion.7
  142.3 3.5 fusion.125
  150.6 3.5 fusion.125
  158.8 3.5 fusion.125
  167.1 3.5 fusion.125
  175.0 3.1 slice_bitcast_fusion
  184.2 32.9 %while.42 = (s32[]{:T(128)}, f32[4,512,2]{1,2,0:T(2,128)S(1)}, f32[4,512,2,128]{3,1,2,0:T(8,128)}, f32[4,512,2]{1,2,0:T(2,128)S(1)}, f32[4,512,2]{1,2,0:T(2,128)...) while((s32[]{:T(128)}, f32[4,512,2]{1,2,0:T(2,128)S(1)}, ...), condition=%wide.region_13.14_spmd, body=%wide.region_10.13_spmd.sunk | while | flops 1094981632 | bytes 32827028 | solution.py:40
  187.0 3.5 fusion.132
  195.2 3.5 fusion.132
  203.5 3.5 fusion.132
  211.7 3.5 fusion.132
  221.5 121.5 %all-gather.2.cloned.1.call-done = bf16[2048,4096]{1,0:T(8,128)(2,1)} async-done(((bf16[2048,256]{1,0:T(8,128)(2,1)}), bf16[2048,4096]{1,0:T(8,128)(2,1)}) %all-gather.2.cloned.1.call-update) | async-done | bytes 16777232 | tf_op jit(solution)/shard_map/all_gather | solution.py:90
  343.1 13.2 %convolution_convert_fusion = bf16[2048,384]{1,0:T(8,128)(2,1)} fusion(bf16[2048,4096]{1,0:T(8,128)(2,1)} %all-gather.2.cloned.1.call-done, bf16[4096,384]{1,0:T(8,128)(2,1)S(1)} %copy-done), kind=kOutput, calls=%fused_computation.80 | convolution fusion | flops 6443237376 | bytes 21495808 | tf_op jit(solution)/shard_map/dot_general | solution.py:89
  (116 shorter events, 115.1 us)
Async XLA Ops:
  6.5 336.5 %copy-start = (bf16[4096,384]{1,0:T(8,128)(2,1)S(1)}, bf16[4096,384]{1,0:T(8,128)(2,1)}, u32[]{:S(2)}) copy-start(bf16[4096,384]{1,0:T(8,128)(2,1)} %param.14) | copy-start | bytes 9437188
  6.5 54.8 %copy-start.4 = (s32[8,8]{1,0:T(8,128)S(1)}, s32[8,8]{1,0:T(8,128)}, u32[]{:S(2)}) copy-start(s32[8,8]{1,0:T(8,128)} %param.15) | copy-start | bytes 772
  9.0 24.8 %all-to-all-start.1 = ((bf16[128,16,256]{0,2,1:T(8,128)(2,1)}), bf16[128,16,256]{0,2,1:T(8,128)(2,1)}, u32[]{:S(2)}, u32[]{:S(2)}) async-start(bf16[128,16,256]{0,2,1:T(8,128)(2,1)} %bitcast.265), calls=%async_computation.1 | async-start | bytes 2097152 | tf_op jit(solution)/shard_map/all_to_all | solution.py:55
  33.7 22.4 %all-to-all-start.2 = ((bf16[128,16,256]{0,2,1:T(8,128)(2,1)}), bf16[128,16,256]{0,2,1:T(8,128)(2,1)}, u32[]{:S(2)}, u32[]{:S(2)}) async-start(bf16[128,16,256]{0,2,1:T(8,128)(2,1)} %bitcast.263), calls=%async_computation.2 | async-start | bytes 2097152 | tf_op jit(solution)/shard_map/all_to_all | solution.py:56
  56.2 28.5 %all-to-all-start = ((bf16[128,16,256]{2,0,1:T(8,128)(2,1)}), bf16[128,16,256]{2,0,1:T(8,128)(2,1)}, u32[]{:S(2)}, u32[]{:S(2)}) async-start(bf16[128,16,256]{2,0,1:T(8,128)(2,1)} %bitcast.262), calls=%async_computation | async-start | bytes 2097152 | tf_op jit(solution)/shard_map/all_to_all | solution.py:54
  61.2 281.8 %all-gather.2.cloned.1.call-start = ((), (), s32[]{:S(2)}) async-start(), calls=%async_computation.3 | async-start | bytes 17825792 | tf_op jit(solution)/shard_map/all_gather | solution.py:90
  83.2 47.2 %collective-permute-start = (bf16[2,2048,2,128]{1,3,2,0:T(8,128)(2,1)}, bf16[2,2048,2,128]{1,3,2,0:T(8,128)(2,1)}, u32[]{:S(2)}, u32[]{:S(2)}) collective-permute-start(bf16[2,2048,2,128]{1,3,2,0:T(8,128)(2,1)} %constant_dynamic-update-slice_fusion), channel_id=1, source_target_pairs={{0,16},{16,32},{32,48},{48,64},{64,80},{80,96},{96,112},{112,0},{1... | collective-permute-start | bytes 6291464 | tf_op jit(solution)/shard_map/ppermute | solution.py:13
  83.9 91.1 %collective-permute-start.1 = (bf16[2,2048,2,128]{1,3,2,0:T(8,128)(2,1)}, bf16[2,2048,2,128]{1,3,2,0:T(8,128)(2,1)}, u32[]{:S(2)}, u32[]{:S(2)}) collective-permute-start(bf16[2,2048,2,128]{1,3,2,0:T(8,128)(2,1)} %constant_dynamic-update-slice_fusion), channel_id=1, source_target_pairs={{0,112},{16,0},{32,16},{48,32},{64,48},{80,64},{96,80},{112,96},{1... | collective-permute-start | bytes 6291464 | tf_op jit(solution)/shard_map/ppermute | solution.py:13
  95.2 2.8 copy-start.3
  102.2 2.8 copy-start.3
  109.2 2.8 copy-start.3
  116.2 2.8 copy-start.3
  139.5 2.8 copy-start.1
  147.8 2.8 copy-start.1
  156.1 2.8 copy-start.1
  164.3 2.8 copy-start.1
  184.2 2.8 copy-start.2
  192.4 2.8 copy-start.2
  200.7 2.8 copy-start.2
  208.9 2.8 copy-start.2
Sparse Core Ops, SparseCore 0:
  221.7 121.3 all-gather.1
where the time goes:
time: 367 us; the launch traced here: 363 us
  waiting for transfers between devices  161 us (44%)
  matrix products  84.2 us (23%)
  local copies, waits for them, and re-layouts  57.8 us (16%)
  other arithmetic  25.2 us (7%)
  starting transfers between devices  19.3 us (5%)
  between operations  14.9 us (4%)
    all_gather x1, waiting for transfers between devices, body(): lax.all_gather(attended, 'space', axis=1, tiled=True)  122 us
    dot_general x12, matrix products, one_block(): jnp.einsum('qhk,khd->qhd', exp_terms.astype(jnp.bfloat16), values_here, p...  38.2 us
    dot_general x12, matrix products, one_block(): jnp.einsum('qhd,khd->qhk', query_part, keys_here, preferred_element_type=...  32.7 us
    reduce_sum x12, other arithmetic, one_block(): new_total = old_total * rescale + jnp.sum(exp_terms, axis=2)  21.8 us
    while x7, local copies, waits for them, and re-layouts, block_update(): return lax.map(one_block, (query_blocks, run_max, run_total, run_sum))  15.9 us
    all_to_all x1, waiting for transfers between devices, body(): lax.all_to_all(value_vectors, 'space', split_axis=1, concat_axis=0, tiled...  15 us
    all_to_all x1, waiting for transfers between devices, body(): lax.all_to_all(key_vectors, 'space', split_axis=1, concat_axis=0, tiled=T...  14.9 us
    dot_general x1, matrix products, body(): jnp.dot(lax.all_gather(attended, 'space', axis=1, tiled=True), out_weight...  13.2 us
  transfers between devices with their start and end apart: 6, of which 5 were waited for; matrix products, arithmetic and copies ran while one was open for 29% of the time, Pallas kernels for 0%

commit v1 on v0

v1 whole, which is shorter than its diff:
```python
import functools
import math

import jax
import jax.numpy as jnp
from jax import lax
from jax.experimental import pallas as pl
from jax.experimental.pallas import tpu as pltpu
from jax.sharding import PartitionSpec as P

MESH = pl.DeviceIdType.MESH
HD = 128
HEADS = 32
TOK = 128
BT = 2048
TQ = 256
KC = 512
SLOPE = math.log2(math.e) / math.sqrt(HD)
BIG = 1e30


def place():
    tm = lax.axis_index("tm")
    sp = lax.axis_index("space")
    return tm, sp, tm // 2, tm % 2


def taken(ref, sem):
    pltpu.make_async_copy(ref, ref, sem).wait()


def attend_tile(q, k_all, v_all, scores, base, bits):
    chunks = BT // KC
    top = None
    for j in range(3):
        part = None
        for c in range(chunks):
            off = j * BT + c * KC
            s = lax.dot_general(
                q, k_all[pl.ds(base + off, KC), :], (((1,), (1,)), ((), ())),
                preferred_element_type=jnp.float32,
            )
            scores[:, off:off + KC] = s
            for lane in range(0, KC, 128):
                piece = s[:, lane:lane + 128]
                part = piece if part is None else jnp.maximum(part, piece)
        if bits[j] is not None:
            part = jnp.where(bits[j], part, -jnp.inf)
        top = part if top is None else jnp.maximum(top, part)
    top = jnp.max(top, axis=1, keepdims=True)
    acc = None
    total = None
    for j in range(3):
        sub = top if bits[j] is None else jnp.where(bits[j], top, BIG)
        for c in range(chunks):
            off = j * BT + c * KC
            p = jnp.exp2((scores[:, off:off + KC] - sub) * SLOPE)
            for lane in range(0, KC, 128):
                piece = p[:, lane:lane + 128]
                total = piece if total is None else total + piece
            d = jnp.dot(
                p.astype(jnp.bfloat16), v_all[pl.ds(base + off, KC), :],
                preferred_element_type=jnp.float32,
            )
            acc = d if acc is None else acc + d
    return (acc / jnp.sum(total, axis=1, keepdims=True)).astype(jnp.bfloat16)


def exchange_kernel(
    q_src, k_src, v_src, q_hbm, k_hbm, v_hbm, mask_ref, att_ref,
    q_all, k_all, v_all, scores, sent, landed, passed_sem, came_sem,
):
    tm, sp, y, xl = place()
    me = xl * 16 + sp
    up = ((y + 1) % 4) * 2 + xl
    down = ((y + 3) % 4) * 2 + xl

    barrier = pltpu.get_barrier_semaphore()

    def greet(i, carry):
        p = (me + i) % 32
        pl.semaphore_signal(barrier, inc=1, device_id=(y * 2 + p // 16, p % 16), device_id_type=MESH)
        return carry

    lax.fori_loop(1, 32, greet, 0)
    pl.semaphore_signal(barrier, inc=1, device_id=(up, sp), device_id_type=MESH)
    pl.semaphore_signal(barrier, inc=1, device_id=(down, sp), device_id_type=MESH)
    pl.semaphore_wait(barrier, 33)

    mine = pl.ds(pl.multiple_of((sp * 2 + xl) * HD, HD), HD)
    plan = ((k_src, k_hbm, k_all, BT), (v_src, v_hbm, v_all, BT), (q_src, q_hbm, q_all, 0))
    for n, (src, hbm, dst, first) in enumerate(plan):
        rows = pl.ds(pl.multiple_of(first + me * TOK, TOK), TOK)
        pltpu.make_async_copy(hbm.at[:, mine], dst.at[rows, :], landed.at[n]).start()

        def send(i, carry, src=src, dst=dst, rows=rows, n=n):
            p = (me + i) % 32
            theirs = pl.ds(pl.multiple_of(((p % 16) * 2 + p // 16) * HD, HD), HD)
            pltpu.make_async_remote_copy(
                src_ref=src.at[:, theirs], dst_ref=dst.at[rows, :],
                send_sem=sent.at[n], recv_sem=landed.at[n],
                device_id=(y * 2 + p // 16, p % 16), device_id_type=MESH,
            ).start()
            return carry

        lax.fori_loop(1, 32, send, 0)

    hops = []
    for n, buf in enumerate((k_all, v_all)):
        taken(buf.at[BT:3 * BT, :], landed.at[n])
        for way, (there, src, dst) in enumerate(((up, 2 * BT, 0), (down, BT, 3 * BT))):
            hop = pltpu.make_async_remote_copy(
                src_ref=buf.at[src:src + BT, :], dst_ref=buf.at[dst:dst + BT, :],
                send_sem=passed_sem.at[2 * n + way], recv_sem=came_sem.at[2 * n + way],
                device_id=(there, sp), device_id_type=MESH,
            )
            hop.start()
            hops.append(hop)
    taken(q_all, landed.at[2])
    for hop in hops:
        hop.wait()
    for n in range(3):
        taken(q_all.at[0:31 * TOK, :], sent.at[n])

    per = BT // TQ

    def tile(t, carry):
        half = t // per
        block = y * 2 + half
        before = mask_ref[block, (block + 7) % 8] == 1
        after = mask_ref[block, (block + 1) % 8] == 1
        rows = pl.ds(pl.multiple_of(t * TQ, TQ), TQ)
        base = pl.multiple_of(half * BT, BT)
        att_ref[rows, :] = attend_tile(q_all[rows, :], k_all, v_all, scores, base, (before, None, after))
        return carry

    lax.fori_loop(0, 2 * per, tile, 0)


def exchange_and_attend(queries, key_vectors, value_vectors, frame_mask):
    vmem = pl.BlockSpec(memory_space=pltpu.VMEM)
    hbm = pl.BlockSpec(memory_space=pl.ANY)
    return pl.pallas_call(
        exchange_kernel,
        name="exchange_attend",
        out_shape=jax.ShapeDtypeStruct((2 * BT, HD), jnp.bfloat16),
        in_specs=[vmem] * 3 + [hbm] * 3 + [pl.BlockSpec(memory_space=pltpu.SMEM)],
        out_specs=vmem,
        scratch_shapes=[
            pltpu.VMEM((2 * BT, HD), jnp.bfloat16),
            pltpu.VMEM((4 * BT, HD), jnp.bfloat16),
            pltpu.VMEM((4 * BT, HD), jnp.bfloat16),
            pltpu.VMEM((TQ, 3 * BT), jnp.float32),
            pltpu.SemaphoreType.DMA((3,)),
            pltpu.SemaphoreType.DMA((3,)),
            pltpu.SemaphoreType.DMA((4,)),
            pltpu.SemaphoreType.DMA((4,)),
        ],
        compiler_params=pltpu.CompilerParams(
            collective_id=0, has_side_effects=True, vmem_limit_bytes=48 * 2**20
        ),
        cost_estimate=pl.CostEstimate(flops=13 * 10**9, bytes_accessed=8 * 2**20, transcendentals=25 * 10**6),
    )(queries, key_vectors, value_vectors, queries, key_vectors, value_vectors, frame_mask)


ROWS = BT // 2
COLS = 384
PART = 256


def project_kernel(
    att_hbm, w_hbm, out_ref, got, w_all, acc, theirs,
    near_send, near_recv, far_send, far_recv, relay_send, relay_recv, w_mine, w_send, w_recv, o_send, o_recv,
):
    tm, sp, y, xl = place()
    z = sp // 4
    xh = (sp // 2) % 2
    core = sp % 2
    head = sp * 2 + xl
    above = ((z + 1) % 4) * 4 + xh * 2 + core
    below = ((z + 3) % 4) * 4 + xh * 2 + core
    partner = sp + 1 - 2 * core

    barrier = pltpu.get_barrier_semaphore()
    near = xh * 4 + core * 2 + xl

    def row_device(p):
        return (y * 2 + p % 2, z * 4 + (p // 4) * 2 + (p // 2) % 2)

    def greet(i, carry):
        pl.semaphore_signal(barrier, inc=1, device_id=row_device((near + i) % 8), device_id_type=MESH)
        return carry

    lax.fori_loop(1, 8, greet, 0)
    pl.semaphore_signal(barrier, inc=1, device_id=(tm, above), device_id_type=MESH)
    pl.semaphore_signal(barrier, inc=1, device_id=(tm, below), device_id_type=MESH)
    pl.semaphore_wait(barrier, 9)

    def rows_of(p):
        quarter = (p % 2) * 2 + (p // 2) % 2
        return pl.ds(pl.multiple_of(quarter * ROWS, ROWS), ROWS)

    own = pltpu.make_async_copy(att_hbm.at[rows_of(near), :], got.at[head], near_recv.at[near])
    own.start()

    def send(i, carry):
        p = (near + i) % 8
        pltpu.make_async_remote_copy(
            src_ref=att_hbm.at[rows_of(p), :], dst_ref=got.at[head],
            send_sem=near_send, recv_sem=near_recv.at[near],
            device_id=row_device(p), device_id_type=MESH,
        ).start()
        return carry

    lax.fori_loop(1, 8, send, 0)

    mine = pl.ds(pl.multiple_of(core * COLS, COLS), COLS)
    w_own = pltpu.make_async_copy(w_hbm, w_all.at[:, mine], w_mine)
    w_own.start()
    w_copy = pltpu.make_async_remote_copy(
        src_ref=w_hbm, dst_ref=w_all.at[:, mine], send_sem=w_send, recv_sem=w_recv,
        device_id=(tm, partner), device_id_type=MESH,
    )
    w_copy.start()

    def onward(i, carry):
        p = (near + i) % 8
        slot = z * 8 + p
        taken(got.at[slot], near_recv.at[p])
        for way, there in enumerate((above, below)):
            pltpu.make_async_remote_copy(
                src_ref=got.at[slot], dst_ref=got.at[slot],
                send_sem=far_send, recv_sem=far_recv.at[way, p],
                device_id=(tm, there), device_id_type=MESH,
            ).start()
        return carry

    lax.fori_loop(0, 8, onward, 0)

    z_from_below = (z + 3) % 4
    z_from_above = (z + 1) % 4
    z_far = (z + 2) % 4

    w_own.wait()
    w_copy.wait()
    half = pl.multiple_of(core * ROWS, ROWS)
    cut = [pl.ds(pl.multiple_of(c * COLS, COLS), COLS) for c in (core, 1 - core)]

    def product(zz, first=False, last=False):
        def rows(r, carry):
            part = pl.ds(pl.multiple_of(r * PART, PART), PART)
            lhs = jnp.concatenate([got[zz * 8 + i, part, :] for i in range(8)], axis=1)
            k_rows = pl.ds(pl.multiple_of(zz * 1024, 1024), 1024)
            d = jnp.dot(lhs, w_all[k_rows, :], preferred_element_type=jnp.float32)
            acc[part, :] = d if first else acc[part, :] + d
            if last:
                theirs[part, :] = acc[part, cut[1]].astype(jnp.bfloat16)
                out_ref[pl.ds(pl.multiple_of(half + r * PART, PART), PART), :] = acc[part, cut[0]].astype(jnp.bfloat16)
            return carry

        lax.fori_loop(0, ROWS // PART, rows, 0)

    product(z, first=True)

    def pass_on(i, carry):
        for way, (zz, there) in enumerate(((z_from_below, above), (z_from_above, below))):
            p = i + 4 * way
            slot = zz * 8 + p
            taken(got.at[slot], far_recv.at[way, p])
            pltpu.make_async_remote_copy(
                src_ref=got.at[slot], dst_ref=got.at[slot],
                send_sem=relay_send, recv_sem=relay_recv,
                device_id=(tm, there), device_id_type=MESH,
            ).start()
        return carry

    lax.fori_loop(0, 4, pass_on, 0)

    def rest(i, carry):
        for way, zz in enumerate((z_from_below, z_from_above)):
            p = i + 4 * (1 - way)
            taken(got.at[zz * 8 + p], far_recv.at[way, p])
        return carry

    lax.fori_loop(0, 4, rest, 0)
    product(z_from_below)
    product(z_from_above)
    taken(got.at[pl.ds(z_far * 8, 8)], relay_recv)
    product(z_far, last=True)
    o_copy = pltpu.make_async_remote_copy(
        src_ref=theirs, dst_ref=out_ref.at[pl.ds(half, ROWS), :], send_sem=o_send, recv_sem=o_recv,
        device_id=(tm, partner), device_id_type=MESH,
    )
    o_copy.start()
    o_copy.wait()
    taken(got.at[0:7], near_send)
    taken(got.at[0:16], far_send)
    taken(got.at[0:8], relay_send)


def gather_and_project(att, out_weight):
    vmem = pl.BlockSpec(memory_space=pltpu.VMEM)
    hbm = pl.BlockSpec(memory_space=pl.ANY)
    dma = pltpu.SemaphoreType.DMA
    return pl.pallas_call(
        project_kernel,
        name="gather_project",
        out_shape=jax.ShapeDtypeStruct((BT, COLS), jnp.bfloat16),
        in_specs=[hbm, hbm],
        out_specs=vmem,
        scratch_shapes=[
            pltpu.VMEM((HEADS, ROWS, HD), jnp.bfloat16),
            pltpu.VMEM((HEADS * HD, 2 * COLS), jnp.bfloat16),
            pltpu.VMEM((ROWS, 2 * COLS), jnp.float32),
            pltpu.VMEM((ROWS, COLS), jnp.bfloat16),
            dma, dma((8,)), dma, dma((2, 8)), dma, dma, dma, dma, dma, dma, dma,
        ],
        compiler_params=pltpu.CompilerParams(
            collective_id=1, has_side_effects=True, vmem_limit_bytes=48 * 2**20
        ),
        cost_estimate=pl.CostEstimate(flops=64 * 10**8, bytes_accessed=8 * 2**20, transcendentals=0),
    )(att, out_weight)


def body(queries, key_vectors, value_vectors, out_weight, frame_mask):
    att = exchange_and_attend(queries, key_vectors, value_vectors, frame_mask)
    return gather_and_project(att, out_weight)


def solution(mesh):
    in_specs = (
        P(("tm", "space"), None),
        P(("tm", "space"), None),
        P(("tm", "space"), None),
        P(None, "space"),
        P(),
    )
    return jax.shard_map(body, mesh=mesh, in_specs=in_specs, out_specs=P("tm", "space"), check_vma=False)
```

time: 367 us -> 202 us (0.55)
  the two profiles are of different devices: /device:TPU:27 before, /device:TPU:5 now
where the time goes in v1:
time: 202 us
  Pallas kernels  196 us (97%)
  local copies, waits for them, and re-layouts  5.66 us (3%)
    pallas_call x1, Pallas kernels, gather_and_project(): pl.pallas_call(project_kernel, name='gather_project', out_shape=jax.Shape...  99.8 us
    pallas_call x1, Pallas kernels, exchange_and_attend(): pl.pallas_call(exchange_kernel, name='exchange_attend', out_shape=jax.Sha...  96.2 us
    unnamed x11, local copies, waits for them, and re-layouts  5.66 us

profile of v1, /device:TPU:5, one launch (start us, length us, event | category | flops | bytes accessed | tf_op | source)
XLA Modules:
  0.0 201.7 jit_solution(7334190404221815590)
XLA Ops:
  0.0 0.0 copy-start
  0.0 0.0 copy-start.1
  0.0 1.4 copy-done.1
  1.4 0.0 copy-start.2
  1.4 1.2 copy-done.2
  2.6 0.0 copy-start.3
  2.6 1.2 copy-done.3
  3.8 0.0 copy-start.4
  3.8 0.7 copy-done.4
  4.5 96.2 %exchange_attend.1.att_hbm = bf16[4096,128]{1,0:T(8,128)(2,1)S(1)} custom-call(bf16[128,4096]{1,0:T(8,128)(2,1)S(1)} %copy-done.1, bf16[128,4096]{1,0:T(8,128)(2,1)S(1)} %copy-done.2, bf16[128,4096]{1,0:T(8,128)(2,1)S(1)} %copy-done.3, bf16[128,4096]{1,0:T(8,128)(2,1)S(1)} %copy-done.1, bf16[128,4096]{1,0:T(8,128)(2,1)S(1)} %copy-done.2, ...), custom_call_target="tpu_custom_call" | custom-call | flops 12999999488 | bytes 8388608 | tf_op jit(solution)/shard_map/exchange_attend/pallas_call | solution.py:143
  100.8 0.0 copy-done
  100.8 99.8 %gather_project.1 = bf16[2048,384]{1,0:T(8,128)(2,1)S(1)} custom-call(bf16[4096,128]{1,0:T(8,128)(2,1)S(1)} %exchange_attend.1.att_hbm, bf16[4096,384]{1,0:T(8,128)(2,1)S(1)} %copy-done), custom_call_target="tpu_custom_call" | custom-call | flops 6400000000 | bytes 8388608 | tf_op jit(solution)/shard_map/gather_project/pallas_call | solution.py:305
  200.6 1.1 copy.7
Async XLA Ops:
  0.0 100.8 %copy-start = (bf16[4096,384]{1,0:T(8,128)(2,1)S(1)}, bf16[4096,384]{1,0:T(8,128)(2,1)}, u32[]{:S(2)}) copy-start(bf16[4096,384]{1,0:T(8,128)(2,1)} %w_hbm.1) | copy-start | bytes 9437188
  0.0 1.4 copy-start.1
  1.4 1.2 copy-start.2
  2.6 1.2 copy-start.3
  3.8 0.7 copy-start.4

commit v2 on v1

v2 whole, which is shorter than its diff:
```python
import functools
import math

import jax
import jax.numpy as jnp
from jax import lax
from jax.experimental import pallas as pl
from jax.experimental.pallas import tpu as pltpu
from jax.sharding import PartitionSpec as P

MESH = pl.DeviceIdType.MESH
HD = 128
HEADS = 32
TOK = 128
BT = 2048
TQ = 256
KC = 512
COLS = 384
ROWS = 512
STEPS = 16
SLOPE = math.log2(math.e) / math.sqrt(HD)
BIG = 1e30


def place():
    tm = lax.axis_index("tm")
    sp = lax.axis_index("space")
    return tm, sp, tm // 2, tm % 2


def taken(ref, sem):
    pltpu.make_async_copy(ref, ref, sem).wait()


def attend_tile(q, k_all, v_all, scores, base, bits):
    chunks = BT // KC
    top = None
    for j in range(3):
        part = None
        for c in range(chunks):
            off = j * BT + c * KC
            s = lax.dot_general(
                q, k_all[pl.ds(base + off, KC), :], (((1,), (1,)), ((), ())),
                preferred_element_type=jnp.float32,
            )
            scores[:, off:off + KC] = s
            for lane in range(0, KC, 128):
                piece = s[:, lane:lane + 128]
                part = piece if part is None else jnp.maximum(part, piece)
        if bits[j] is not None:
            part = jnp.where(bits[j], part, -jnp.inf)
        top = part if top is None else jnp.maximum(top, part)
    top = jnp.max(top, axis=1, keepdims=True)
    acc = None
    total = None
    for j in range(3):
        sub = top if bits[j] is None else jnp.where(bits[j], top, BIG)
        for c in range(chunks):
            off = j * BT + c * KC
            p = jnp.exp2((scores[:, off:off + KC] - sub) * SLOPE)
            for lane in range(0, KC, 128):
                piece = p[:, lane:lane + 128]
                total = piece if total is None else total + piece
            d = jnp.dot(
                p.astype(jnp.bfloat16), v_all[pl.ds(base + off, KC), :],
                preferred_element_type=jnp.float32,
            )
            acc = d if acc is None else acc + d
    return (acc / jnp.sum(total, axis=1, keepdims=True)).astype(jnp.bfloat16)


def kernel(
    q_src, k_src, v_src, q_hbm, k_hbm, v_hbm, w_hbm, mask_ref, out_ref,
    q_all, k_all, v_all, scores, att, got, w_all, done,
    sent, landed, passed_sem, came_sem, near_send, near_recv, far_send, far_recv,
    w_mine, w_send, w_recv, o_send, o_recv,
):
    tm, sp, y, xl = place()
    z = sp // 4
    xh = (sp // 2) % 2
    core = sp % 2
    me = xl * 16 + sp

    def at_y(step):
        return (((y + step) % 4) * 2 + xl, sp)

    def at_z(step):
        return (tm, ((z + step) % 4) * 4 + sp % 4)

    barrier = pltpu.get_barrier_semaphore()

    def greet(i, carry):
        p = (me + i) % 32
        pl.semaphore_signal(barrier, inc=1, device_id=(y * 2 + p // 16, p % 16), device_id_type=MESH)
        return carry

    lax.fori_loop(1, 32, greet, 0)
    for step in (1, 2, 3):
        pl.semaphore_signal(barrier, inc=1, device_id=at_y(step), device_id_type=MESH)
    pl.semaphore_wait(barrier, 34)

    mine = pl.ds(pl.multiple_of((sp * 2 + xl) * HD, HD), HD)
    plan = ((k_src, k_hbm, k_all, BT), (v_src, v_hbm, v_all, BT), (q_src, q_hbm, q_all, 0))
    for n, (src, hbm, dst, first) in enumerate(plan):
        rows = pl.ds(pl.multiple_of(first + me * TOK, TOK), TOK)
        pltpu.make_async_copy(hbm.at[:, mine], dst.at[rows, :], landed.at[n]).start()

        def send(i, carry, src=src, dst=dst, rows=rows, n=n):
            p = (me + i) % 32
            theirs = pl.ds(pl.multiple_of(((p % 16) * 2 + p // 16) * HD, HD), HD)
            pltpu.make_async_remote_copy(
                src_ref=src.at[:, theirs], dst_ref=dst.at[rows, :],
                send_sem=sent.at[n], recv_sem=landed.at[n],
                device_id=(y * 2 + p // 16, p % 16), device_id_type=MESH,
            ).start()
            return carry

        lax.fori_loop(1, 32, send, 0)

    def columns(g):
        return pl.ds(pl.multiple_of(g * COLS, COLS), COLS)

    g_me = xh * 2 + core
    g_far = (1 - xh) * 2 + core
    quarter = pl.ds(pl.multiple_of(y * 1024, 1024), 1024)
    partner = (tm, sp + 1 - 2 * core)
    across = (y * 2 + 1 - xl, z * 4 + g_far)
    w_own = pltpu.make_async_copy(w_hbm, w_all.at[:, columns(g_me)], w_mine)
    w_own.start()
    w_near = pltpu.make_async_remote_copy(
        src_ref=w_hbm, dst_ref=w_all.at[:, columns(g_me)], send_sem=w_send.at[0], recv_sem=w_recv.at[0],
        device_id=partner, device_id_type=MESH,
    )
    w_near.start()
    w_first = pltpu.make_async_remote_copy(
        src_ref=w_hbm.at[quarter, :], dst_ref=w_all.at[quarter, columns(g_me)],
        send_sem=w_send.at[1], recv_sem=w_recv.at[1], device_id=across, device_id_type=MESH,
    )
    w_first.start()

    hops = []
    for n, buf in enumerate((k_all, v_all)):
        taken(buf.at[BT:3 * BT, :], landed.at[n])
        for way, (step, src, dst) in enumerate(((1, 2 * BT, 0), (3, BT, 3 * BT))):
            hop = pltpu.make_async_remote_copy(
                src_ref=buf.at[src:src + BT, :], dst_ref=buf.at[dst:dst + BT, :],
                send_sem=passed_sem.at[2 * n + way], recv_sem=came_sem.at[2 * n + way],
                device_id=at_y(step), device_id_type=MESH,
            )
            hop.start()
            hops.append(hop)
    taken(q_all, landed.at[2])
    for hop in hops:
        hop.wait()
    for n in range(3):
        taken(q_all.at[0:31 * TOK, :], sent.at[n])

    turn = core * 4 + xh * 2 + xl
    slot = xh * 4 + core * 2 + xl

    def along_z(chunk):
        rows = pl.ds(chunk * TQ, TQ)
        taken(got.at[0, 0:7, 0:TQ, :], near_recv.at[chunk])
        for step in (1, 3, 2):
            pltpu.make_async_remote_copy(
                src_ref=got.at[z, :, rows, :], dst_ref=got.at[z, :, rows, :],
                send_sem=far_send, recv_sem=far_recv.at[chunk],
                device_id=at_z(step), device_id_type=MESH,
            ).start()

    def tile(s, carry):
        chunk = s // 8
        to_core = (s % 8) // 4
        half = s % 2
        to_xh = (s % 4) // 2
        block = y * 2 + half
        before = mask_ref[block, (block + 7) % 8] == 1
        after = mask_ref[block, (block + 1) % 8] == 1
        rows = pl.ds(pl.multiple_of(half * BT + (to_xh * 2 + to_core) * ROWS + chunk * TQ, TQ), TQ)
        base = pl.multiple_of(half * BT, BT)
        there = pl.ds(pl.multiple_of(chunk * TQ, TQ), TQ)
        result = attend_tile(q_all[rows, :], k_all, v_all, scores, base, (before, None, after))

        @pl.when(s % 8 == turn)
        def _():
            got[z, slot, there, :] = result

        @pl.when(s % 8 != turn)
        def _():
            att[rows, :] = result
            pltpu.make_async_remote_copy(
                src_ref=att.at[rows, :], dst_ref=got.at[z, slot, there, :],
                send_sem=near_send, recv_sem=near_recv.at[chunk],
                device_id=(y * 2 + half, z * 4 + to_xh * 2 + to_core), device_id_type=MESH,
            ).start()

        for c in (0, 1):
            @pl.when(s == c * 8 + turn + 2)
            def _(c=c):
                along_z(c)

        @pl.when(s == 4)
        def _():
            w_first.wait()
            for n, step in enumerate((1, 3, 2)):
                pltpu.make_async_remote_copy(
                    src_ref=w_all.at[quarter, columns(g_far)], dst_ref=w_all.at[quarter, columns(g_far)],
                    send_sem=w_send.at[2], recv_sem=w_recv.at[2], device_id=at_y(step), device_id_type=MESH,
                ).start()

        return carry

    lax.fori_loop(0, STEPS, tile, 0)

    @pl.when(turn >= 6)
    def _():
        along_z(1)

    w_own.wait()
    w_near.wait()
    taken(w_all.at[0:3072, 0:COLS], w_recv.at[2])
    w_last = pltpu.make_async_remote_copy(
        src_ref=w_all.at[:, columns(g_far)], dst_ref=w_all.at[:, columns(g_far)],
        send_sem=w_send.at[3], recv_sem=w_recv.at[3], device_id=partner, device_id_type=MESH,
    )
    w_last.start()
    w_last.wait()

    for chunk in (0, 1):
        rows = pl.ds(chunk * TQ, TQ)
        out_rows = pl.ds(pl.multiple_of(g_me * ROWS + chunk * TQ, TQ), TQ)
        taken(got.at[0:3, :, 0:TQ, :], far_recv.at[chunk])
        lhs = jnp.concatenate([got[i // 8, i % 8, rows, :] for i in range(HEADS)], axis=1)
        for pair in (1, 0):
            side = (xh + pair) % 2
            wide = pl.ds(pl.multiple_of(side * 2 * COLS, 2 * COLS), 2 * COLS)
            d = jnp.dot(lhs, w_all[:, wide], preferred_element_type=jnp.float32).astype(jnp.bfloat16)
            for c in (0, 1):
                g = side * 2 + c
                block = d[:, c * COLS:(c + 1) * COLS]

                @pl.when(g == g_me)
                def _(block=block):
                    out_ref[out_rows, :] = block

                @pl.when(g != g_me)
                def _(block=block, g=g, n=chunk * 4 + pair * 2 + c, c=c, side=side):
                    done[n] = block
                    pltpu.make_async_remote_copy(
                        src_ref=done.at[n], dst_ref=out_ref.at[out_rows, :],
                        send_sem=o_send, recv_sem=o_recv,
                        device_id=(tm, z * 4 + g), device_id_type=MESH,
                    ).start()

    taken(out_ref.at[0:6 * TQ, :], o_recv)
    taken(out_ref.at[0:6 * TQ, :], o_send)
    taken(q_all.at[0:14 * TQ, :], near_send)
    taken(got.at[0:3], far_send)
    taken(w_all.at[0:3072, 0:COLS], w_send.at[2])


def body(queries, key_vectors, value_vectors, out_weight, frame_mask):
    vmem = pl.BlockSpec(memory_space=pltpu.VMEM)
    hbm = pl.BlockSpec(memory_space=pl.ANY)
    dma = pltpu.SemaphoreType.DMA
    bf16 = jnp.bfloat16
    return pl.pallas_call(
        kernel,
        name="layer",
        out_shape=jax.ShapeDtypeStruct((BT, COLS), bf16),
        in_specs=[vmem] * 3 + [hbm] * 4 + [pl.BlockSpec(memory_space=pltpu.SMEM)],
        out_specs=vmem,
        scratch_shapes=[
            pltpu.VMEM((2 * BT, HD), bf16),
            pltpu.VMEM((4 * BT, HD), bf16),
            pltpu.VMEM((4 * BT, HD), bf16),
            pltpu.VMEM((TQ, 3 * BT), jnp.float32),
            pltpu.VMEM((2 * BT, HD), bf16),
            pltpu.VMEM((4, 8, ROWS, HD), bf16),
            pltpu.VMEM((HEADS * HD, 4 * COLS), bf16),
            pltpu.VMEM((8, TQ, COLS), bf16),
            dma((3,)), dma((3,)), dma((4,)), dma((4,)), dma, dma((2,)), dma, dma((2,)),
            dma, dma((4,)), dma((4,)), dma, dma,
        ],
        compiler_params=pltpu.CompilerParams(
            collective_id=0, has_side_effects=True, vmem_limit_bytes=60 * 2**20
        ),
        cost_estimate=pl.CostEstimate(flops=19 * 10**9, bytes_accessed=8 * 2**20, transcendentals=25 * 10**6),
    )(queries, key_vectors, value_vectors, queries, key_vectors, value_vectors, out_weight, frame_mask)


def solution(mesh):
    in_specs = (
        P(("tm", "space"), None),
        P(("tm", "space"), None),
        P(("tm", "space"), None),
        P(None, "space"),
        P(),
    )
    return jax.shard_map(body, mesh=mesh, in_specs=in_specs, out_specs=P("tm", "space"), check_vma=False)
```

time: 202 us -> 141 us (0.70)
  the two profiles are of different devices: /device:TPU:5 before, /device:TPU:27 now
where the time goes in v2:
time: 141 us; the launch traced here: 140 us
  Pallas kernels  137 us (97%)
  local copies, waits for them, and re-layouts  2.71 us (2%)
    pallas_call x1, Pallas kernels, body(): pl.pallas_call(kernel, name='layer', out_shape=jax.ShapeDtypeStruct((BT,...  137 us

profile of v2, /device:TPU:27, one launch (start us, length us, event | category | flops | bytes accessed | tf_op | source)
XLA Modules:
  0.0 139.7 jit_solution(577142571327467549)
XLA Ops:
  0.0 137.0 %layer.1 = bf16[2048,384]{1,0:T(8,128)(2,1)} custom-call(bf16[128,4096]{1,0:T(8,128)(2,1)} %q_hbm.1, bf16[128,4096]{1,0:T(8,128)(2,1)} %k_hbm.1, bf16[128,4096]{1,0:T(8,128)(2,1)} %v_hbm.1, bf16[128,4096]{1,0:T(8,128)(2,1)} %q_hbm.1, bf16[128,4096]{1,0:T(8,128)(2,1)} %k_hbm.1, bf16[128,4096]{1,0:T(8,128)(2,1)} %v_hbm.1, bf16[4096,384]{1,0:T(8,128)(2,1)} %w_hbm.1, ...), custom_call_target="tpu_custom_call" | custom-call | flops 19000000512 | bytes 8388608 | tf_op jit(solution)/shard_map/layer/pallas_call | solution.py:267
  137.0 2.7 %copy.7 = bf16[2048,384]{1,0:T(8,128)(2,1)} copy(bf16[2048,384]{1,0:T(8,128)(2,1)} %layer.1) | data formatting | bytes 3145728

commit v3 on v2

v3 whole, which is shorter than its diff:
```python
import functools
import math

import jax
import jax.numpy as jnp
from jax import lax
from jax.experimental import pallas as pl
from jax.experimental.pallas import tpu as pltpu
from jax.sharding import PartitionSpec as P

MESH = pl.DeviceIdType.MESH
HD = 128
HEADS = 32
TOK = 128
BT = 2048
TQ = 256
KC = 512
COLS = 384
ROWS = 512
STEPS = 16
EARLY = 6
RELAY = 4
SLOPE = math.log2(math.e) / math.sqrt(HD)
BIG = 1e30


def place():
    tm = lax.axis_index("tm")
    sp = lax.axis_index("space")
    return tm, sp, tm // 2, tm % 2


def taken(ref, sem):
    pltpu.make_async_copy(ref, ref, sem).wait()


def attend(q, k_all, v_all, scores, blocks, known=None):
    chunks = BT // KC
    top = None
    for j, (base, bit) in enumerate(blocks):
        part = None
        for c in range(chunks):
            off = j * BT + c * KC
            s = lax.dot_general(
                q, k_all[pl.ds(base + c * KC, KC), :], (((1,), (1,)), ((), ())),
                preferred_element_type=jnp.float32,
            )
            scores[:, off:off + KC] = s
            for lane in range(0, KC, 128):
                piece = s[:, lane:lane + 128]
                part = piece if part is None else jnp.maximum(part, piece)
        if bit is not None:
            part = jnp.where(bit, part, -jnp.inf)
        top = part if top is None else jnp.maximum(top, part)
    top = jnp.max(top, axis=1, keepdims=True)
    acc = None
    total = None
    if known is not None:
        old_top, total, acc = known
        top = jnp.maximum(top, old_top[:, 0:1])
        shrink = jnp.exp2((old_top - top) * SLOPE)
        total = total * shrink
        acc = acc * shrink
    for j, (base, bit) in enumerate(blocks):
        sub = top if bit is None else jnp.where(bit, top, BIG)
        for c in range(chunks):
            off = j * BT + c * KC
            p = jnp.exp2((scores[:, off:off + KC] - sub) * SLOPE)
            for lane in range(0, KC, 128):
                piece = p[:, lane:lane + 128]
                total = piece if total is None else total + piece
            d = jnp.dot(
                p.astype(jnp.bfloat16), v_all[pl.ds(base + c * KC, KC), :],
                preferred_element_type=jnp.float32,
            )
            acc = d if acc is None else acc + d
    return top, total, acc


def finish(total, acc):
    return (acc / jnp.sum(total, axis=1, keepdims=True)).astype(jnp.bfloat16)


def kernel(
    q_hbm, k_hbm, v_hbm, w_hbm, mask_ref, out_ref,
    q_all, k_all, v_all, scores, att, got, w_all, done, tile_out, early_top, early_total, early_acc,
    sent, landed, passed_sem, came_sem, near_send, near_recv, far_send, far_recv, relay_recv,
    w_mine, w_send, w_recv, o_send, o_recv, o_own,
):
    tm, sp, y, xl = place()
    z = sp // 4
    xh = (sp // 2) % 2
    core = sp % 2
    me = xl * 16 + sp

    def at_y(step):
        return (((y + step) % 4) * 2 + xl, sp)

    def at_z(step):
        return (tm, ((z + step) % 4) * 4 + sp % 4)

    barrier = pltpu.get_barrier_semaphore()

    def greet(i, carry):
        p = (me + i) % 32
        pl.semaphore_signal(barrier, inc=1, device_id=(y * 2 + p // 16, p % 16), device_id_type=MESH)
        return carry

    lax.fori_loop(1, 32, greet, 0)
    for step in (1, 2, 3):
        pl.semaphore_signal(barrier, inc=1, device_id=at_y(step), device_id_type=MESH)
    pl.semaphore_wait(barrier, 34)

    mine = pl.ds(pl.multiple_of((sp * 2 + xl) * HD, HD), HD)
    plan = ((k_hbm, k_all, BT), (v_hbm, v_all, BT), (q_hbm, q_all, 0))
    cuts = (1, 16, 32)

    def rows_at(n):
        return pl.ds(pl.multiple_of(plan[n][2] + me * TOK, TOK), TOK)

    def send_part(n, part):
        hbm, dst, first = plan[n]

        def send(i, carry):
            p = (me + i) % 32
            theirs = pl.ds(pl.multiple_of(((p % 16) * 2 + p // 16) * HD, HD), HD)
            pltpu.make_async_remote_copy(
                src_ref=hbm.at[:, theirs], dst_ref=dst.at[rows_at(n), :],
                send_sem=sent.at[n, part], recv_sem=landed.at[n],
                device_id=(y * 2 + p // 16, p % 16), device_id_type=MESH,
            ).start()
            return carry

        lax.fori_loop(cuts[part], cuts[part + 1], send, 0)

    def sent_part(n, part):
        taken(q_all.at[0:(cuts[part + 1] - cuts[part]) * TOK, :], sent.at[n, part])

    hops = []

    def hop_on(n):
        buf = plan[n][1]
        taken(buf.at[BT:3 * BT, :], landed.at[n])
        for way, (step, src, dst) in enumerate(((1, 2 * BT, 0), (3, BT, 3 * BT))):
            hop = pltpu.make_async_remote_copy(
                src_ref=buf.at[src:src + BT, :], dst_ref=buf.at[dst:dst + BT, :],
                send_sem=passed_sem.at[2 * n + way], recv_sem=came_sem.at[2 * n + way],
                device_id=at_y(step), device_id_type=MESH,
            )
            hop.start()
            hops.append(hop)

    for n in range(3):
        pltpu.make_async_copy(plan[n][0].at[:, mine], plan[n][1].at[rows_at(n), :], landed.at[n]).start()
    send_part(0, 0)
    send_part(0, 1)
    for n in (0, 1):
        sent_part(n, 0)
        send_part(n + 1, 0)
        sent_part(n, 1)
        send_part(n + 1, 1)
        hop_on(n)

    def columns(n):
        return pl.ds(pl.multiple_of(n * COLS, COLS), COLS)

    near_cols = columns(2 + core)
    far_cols = columns(core)
    quarter = pl.ds(pl.multiple_of(y * 1024, 1024), 1024)
    g_me = xh * 2 + core
    partner = (tm, sp + 1 - 2 * core)
    across = (y * 2 + 1 - xl, z * 4 + (1 - xh) * 2 + core)
    w_first = pltpu.make_async_remote_copy(
        src_ref=w_hbm.at[quarter, :], dst_ref=w_all.at[quarter, far_cols],
        send_sem=w_send.at[1], recv_sem=w_recv.at[1], device_id=across, device_id_type=MESH,
    )
    w_first.start()
    w_own = pltpu.make_async_copy(w_hbm, w_all.at[:, near_cols], w_mine)
    w_own.start()
    w_near = pltpu.make_async_remote_copy(
        src_ref=w_hbm, dst_ref=w_all.at[:, near_cols], send_sem=w_send.at[0], recv_sem=w_recv.at[0],
        device_id=partner, device_id_type=MESH,
    )
    w_near.start()
    w_last = pltpu.make_async_remote_copy(
        src_ref=w_all.at[:, far_cols], dst_ref=w_all.at[:, far_cols],
        send_sem=w_send.at[3], recv_sem=w_recv.at[3], device_id=partner, device_id_type=MESH,
    )

    def spot(s):
        half = s % 2
        row = half * BT + ((s % 4) // 2 * 2 + (s % 8) // 4) * ROWS + s // 8 * TQ
        block = y * 2 + half
        before = mask_ref[block, (block + 7) % 8] == 1
        after = mask_ref[block, (block + 1) % 8] == 1
        return half, pl.ds(pl.multiple_of(row, TQ), TQ), before, after

    def early(s, carry):
        half, rows, before, after = spot(s)
        blocks = ((BT, (half == 0) | before), (2 * BT, (half == 1) | after))
        top, total, acc = attend(q_all[rows, :], k_all, v_all, scores, blocks)
        early_top[s] = jnp.broadcast_to(top, (TQ, HD))
        early_total[s] = total
        early_acc[s] = acc
        return carry

    taken(q_all, landed.at[2])
    lax.fori_loop(0, EARLY, early, 0)
    for hop in hops:
        hop.wait()
    sent_part(2, 0)
    sent_part(2, 1)

    turn = core * 4 + xh * 2 + xl
    slot = xh * 4 + core * 2 + xl

    def along_z(chunk):
        rows = pl.ds(chunk * TQ, TQ)
        taken(got.at[0, 0:7, 0:TQ, :], near_recv.at[chunk])
        for way, step in enumerate((1, 3)):
            pltpu.make_async_remote_copy(
                src_ref=got.at[z, :, rows, :], dst_ref=got.at[z, :, rows, :],
                send_sem=far_send, recv_sem=far_recv.at[2 * chunk + way],
                device_id=at_z(step), device_id_type=MESH,
            ).start()

    def relay_z(chunk):
        rows = pl.ds(chunk * TQ, TQ)
        for way, (come, step) in enumerate(((3, 1), (1, 3))):
            taken(got.at[0, :, 0:TQ, :], far_recv.at[2 * chunk + way])
            part = got.at[(z + come) % 4, 4 * way:4 * way + 4, rows, :]
            pltpu.make_async_remote_copy(
                src_ref=part, dst_ref=part, send_sem=far_send, recv_sem=relay_recv.at[chunk],
                device_id=at_z(step), device_id_type=MESH,
            ).start()

    def tile(s, carry):
        chunk = s // 8
        to_core = (s % 8) // 4
        half = s % 2
        to_xh = (s % 4) // 2
        _, rows, before, after = spot(s)
        base = pl.multiple_of(half * BT, BT)
        there = pl.ds(pl.multiple_of(chunk * TQ, TQ), TQ)

        @pl.when(s < EARLY)
        def _():
            n = jnp.minimum(s, EARLY - 1)
            last = pl.multiple_of(half * 3 * BT, BT)
            bit = ((half == 0) & before) | ((half == 1) & after)
            known = (early_top[n], early_total[n], early_acc[n])
            _, total, acc = attend(q_all[rows, :], k_all, v_all, scores, ((last, bit),), known)
            tile_out[...] = finish(total, acc)

        @pl.when(s >= EARLY)
        def _():
            blocks = ((base, before), (base + BT, None), (base + 2 * BT, after))
            _, total, acc = attend(q_all[rows, :], k_all, v_all, scores, blocks)
            tile_out[...] = finish(total, acc)

        result = tile_out[...]

        @pl.when(s % 8 == turn)
        def _():
            got[z, slot, there, :] = result

        @pl.when(s % 8 != turn)
        def _():
            att[rows, :] = result
            pltpu.make_async_remote_copy(
                src_ref=att.at[rows, :], dst_ref=got.at[z, slot, there, :],
                send_sem=near_send, recv_sem=near_recv.at[chunk],
                device_id=(y * 2 + half, z * 4 + to_xh * 2 + to_core), device_id_type=MESH,
            ).start()

        for c in (0, 1):
            @pl.when(s == c * 8 + turn + 1)
            def _(c=c):
                along_z(c)

            @pl.when(s == c * 8 + turn + RELAY)
            def _(c=c):
                relay_z(c)

        @pl.when(s == 2)
        def _():
            w_first.wait()
            for n, step in enumerate((1, 3, 2)):
                pltpu.make_async_remote_copy(
                    src_ref=w_all.at[quarter, far_cols], dst_ref=w_all.at[quarter, far_cols],
                    send_sem=w_send.at[2], recv_sem=w_recv.at[2], device_id=at_y(step), device_id_type=MESH,
                ).start()

        @pl.when(s == STEPS - 2)
        def _():
            taken(w_all.at[0:3072, 0:COLS], w_recv.at[2])
            w_last.start()

        return carry

    lax.fori_loop(0, STEPS, tile, 0)

    @pl.when(turn == 7)
    def _():
        along_z(1)

    w_own.wait()
    w_near.wait()
    w_last.wait()

    own_copies = []
    for chunk in (0, 1):
        rows = pl.ds(chunk * TQ, TQ)
        out_rows = pl.ds(pl.multiple_of(g_me * ROWS + chunk * TQ, TQ), TQ)

        def give(there, cols, chunk=chunk, out_rows=out_rows):
            pltpu.make_async_remote_copy(
                src_ref=done.at[chunk, :, cols], dst_ref=out_ref.at[out_rows, :],
                send_sem=o_send, recv_sem=o_recv,
                device_id=(tm, there), device_id_type=MESH,
            ).start()

        if chunk == 1:
            @pl.when(turn + 8 + RELAY > STEPS - 1)
            def _():
                relay_z(1)

        taken(got.at[0, :, 0:TQ, :], relay_recv.at[chunk])
        lhs = jnp.concatenate([got[i // 8, i % 8, rows, :] for i in range(HEADS)], axis=1)
        for n in range(3):
            wide = slice(n * 512, (n + 1) * 512)
            done[chunk, :, wide] = jnp.dot(lhs, w_all[:, wide], preferred_element_type=jnp.float32).astype(jnp.bfloat16)
            if n == 1:
                for c in (0, 1):
                    give(z * 4 + (1 - xh) * 2 + c, slice(c * COLS, (c + 1) * COLS))
        give(sp + 1 - 2 * core, columns(3 - core))
        own = pltpu.make_async_copy(done.at[chunk, :, near_cols], out_ref.at[out_rows, :], o_own.at[chunk])
        own.start()
        own_copies.append(own)

    for own in own_copies:
        own.wait()
    taken(done.at[:, :, 0:3 * COLS], o_recv)
    taken(done.at[:, :, 0:3 * COLS], o_send)
    taken(q_all.at[0:14 * TQ, :], near_send)
    taken(got.at[0:3], far_send)
    taken(w_all.at[0:3072, 0:COLS], w_send.at[2])


def body(queries, key_vectors, value_vectors, out_weight, frame_mask):
    hbm = pl.BlockSpec(memory_space=pl.ANY)
    dma = pltpu.SemaphoreType.DMA
    bf16 = jnp.bfloat16
    return pl.pallas_call(
        kernel,
        name="layer",
        out_shape=jax.ShapeDtypeStruct((BT, COLS), bf16),
        in_specs=[hbm] * 4 + [pl.BlockSpec(memory_space=pltpu.SMEM)],
        out_specs=hbm,
        scratch_shapes=[
            pltpu.VMEM((2 * BT, HD), bf16),
            pltpu.VMEM((4 * BT, HD), bf16),
            pltpu.VMEM((4 * BT, HD), bf16),
            pltpu.VMEM((TQ, 3 * BT), jnp.float32),
            pltpu.VMEM((2 * BT, HD), bf16),
            pltpu.VMEM((4, 8, ROWS, HD), bf16),
            pltpu.VMEM((HEADS * HD, 4 * COLS), bf16),
            pltpu.VMEM((2, TQ, 4 * COLS), bf16),
            pltpu.VMEM((TQ, HD), bf16),
            pltpu.VMEM((EARLY, TQ, HD), jnp.float32),
            pltpu.VMEM((EARLY, TQ, HD), jnp.float32),
            pltpu.VMEM((EARLY, TQ, HD), jnp.float32),
            dma((3, 2)), dma((3,)), dma((4,)), dma((4,)), dma, dma((2,)), dma, dma((4,)), dma((2,)),
            dma, dma((4,)), dma((4,)), dma, dma, dma((2,)),
        ],
        compiler_params=pltpu.CompilerParams(
            collective_id=0, has_side_effects=True, vmem_limit_bytes=60 * 2**20
        ),
        cost_estimate=pl.CostEstimate(flops=19 * 10**9, bytes_accessed=8 * 2**20, transcendentals=25 * 10**6),
    )(queries, key_vectors, value_vectors, out_weight, frame_mask)


def solution(mesh):
    in_specs = (
        P(("tm", "space"), None),
        P(("tm", "space"), None),
        P(("tm", "space"), None),
        P(None, "space"),
        P(),
    )
    return jax.shard_map(body, mesh=mesh, in_specs=in_specs, out_specs=P("tm", "space"), check_vma=False)
```

time: 141 us -> 140 us (level)
  no operation moved by 1% of the time
where the time goes in v3:
time: 140 us; the launch traced here: 139 us
  Pallas kernels  137 us (98%)
  local copies, waits for them, and re-layouts  2.71 us (2%)
    pallas_call x1, Pallas kernels, body(): pl.pallas_call(kernel, name='layer', out_shape=jax.ShapeDtypeStruct((BT,...  137 us

profile of v3, /device:TPU:27, one launch (start us, length us, event | category | flops | bytes accessed | tf_op | source)
XLA Modules:
  0.0 139.4 jit_solution(7853762778996817806)
XLA Ops:
  0.0 136.7 %layer.1 = bf16[2048,384]{1,0:T(8,128)(2,1)} custom-call(bf16[128,4096]{1,0:T(8,128)(2,1)} %q_hbm.1, bf16[128,4096]{1,0:T(8,128)(2,1)} %k_hbm.1, bf16[128,4096]{1,0:T(8,128)(2,1)} %v_hbm.1, bf16[4096,384]{1,0:T(8,128)(2,1)} %w_hbm.1, s32[8,8]{1,0:T(8,128)} %mask_ref.1), custom_call_target="tpu_custom_call" | custom-call | flops 19000000512 | bytes 8388608 | tf_op jit(solution)/shard_map/layer/pallas_call | solution.py:354
  136.7 2.7 %copy.7 = bf16[2048,384]{1,0:T(8,128)(2,1)} copy(bf16[2048,384]{1,0:T(8,128)(2,1)} %layer.1) | data formatting | bytes 3145728

commit v4 on v3

--- a/solution.py
+++ b/solution.py
@@ -18,7 +18,7 @@
 COLS = 384
 ROWS = 512
 STEPS = 16
-EARLY = 6
+EARLY = 8
 RELAY = 4
 SLOPE = math.log2(math.e) / math.sqrt(HD)
 BIG = 1e30

time: 140 us -> 138 us (0.986)
  Pallas kernels: 137 us -> 135 us
    pallas_call x1, Pallas kernels: 137 us -> 135 us  [body(): pl.pallas_call(kernel, name='layer', out_shape=jax.ShapeDtypeStruct((BT,...]
where the time goes in v4:
time: 138 us
  Pallas kernels  135 us (98%)
  local copies, waits for them, and re-layouts  2.71 us (2%)
    pallas_call x1, Pallas kernels, body(): pl.pallas_call(kernel, name='layer', out_shape=jax.ShapeDtypeStruct((BT,...  135 us

profile of v4, /device:TPU:27, one launch (start us, length us, event | category | flops | bytes accessed | tf_op | source)
XLA Modules:
  0.0 137.6 jit_solution(14237923685948017285)
XLA Ops:
  0.0 134.8 %layer.1 = bf16[2048,384]{1,0:T(8,128)(2,1)} custom-call(bf16[128,4096]{1,0:T(8,128)(2,1)} %q_hbm.1, bf16[128,4096]{1,0:T(8,128)(2,1)} %k_hbm.1, bf16[128,4096]{1,0:T(8,128)(2,1)} %v_hbm.1, bf16[4096,384]{1,0:T(8,128)(2,1)} %w_hbm.1, s32[8,8]{1,0:T(8,128)} %mask_ref.1), custom_call_target="tpu_custom_call" | custom-call | flops 19000000512 | bytes 8388608 | tf_op jit(solution)/shard_map/layer/pallas_call | solution.py:354
  134.9 2.7 %copy.7 = bf16[2048,384]{1,0:T(8,128)(2,1)} copy(bf16[2048,384]{1,0:T(8,128)(2,1)} %layer.1) | data formatting | bytes 3145728
